TPU v7x, 512 devices: a whole 4x8x8 slice. The times are simulated.
512 devices in a mesh: gx: 64 (over z_hi, y, core), gy: 8 (over z_lo, x).
Axes of the slice: x: 4, y: 8, z: 8 (z_hi: 4, z_lo: 2; z = z_hi * 2 + z_lo), core: 2. Of those that a mesh axis runs over, the one named last changes fastest.
Arguments:
- field: bfloat16 [1, 512, 512, 128], P(None, 'gx', 'gy'), may hold values from -6 to 6
- conv_weight: bfloat16 [3, 3, 128, 128], replicated, may hold values from -0.1875 to 0.1875
- qkv_weight: bfloat16 [128, 384], replicated, may hold values from -4 to 4
- out_weight: bfloat16 [128, 128], replicated, may hold values from -0.5 to 0.5
Outputs:
- result: bfloat16 [1, 512, 512, 128], P(None, 'gx', 'gy')
All inputs are finite; a program needn't handle non-finite values.
Results may differ from a plain program's by a relative error of at most 0.0064.
Values may be sent and summed in bfloat16 or wider, within the bound.
No kernel may reach another device: no remote copies, remote signals or barrier semaphores. Data moves between devices by JAX's collectives and lax.ppermute only.
A program may use at most 64 MiB of HBM per device.

v0:
```python
import jax
import jax.numpy as jnp
from jax import lax
from jax.sharding import PartitionSpec as P

HEADS = 4
HEAD = 32


def to_lines(block):
    return lax.all_to_all(block, "gx", split_axis=2, concat_axis=1, tiled=True)


def to_blocks(lines):
    return lax.all_to_all(lines, "gx", split_axis=1, concat_axis=2, tiled=True)


def neighbour_lines(line):
    n_gx, n_gy = (lax.axis_size("gx"), lax.axis_size("gy"))
    count = n_gx * n_gy

    def device(c):
        c = c % count
        return c % n_gx * n_gy + c // n_gx

    from_left = lax.ppermute(line, ("gx", "gy"), [(device(c), device(c + 1)) for c in range(count)])
    from_right = lax.ppermute(
        line, ("gx", "gy"), [(device(c + 1), device(c)) for c in range(count)]
    )
    return (from_left, from_right)


def convolve(columns, conv_weight):
    length, width = (columns.shape[1], columns.shape[2])
    taps = []
    for a in range(3):
        for b in range(3):
            taps.append(jnp.roll(columns[b], 1 - a, axis=0))
    stacked = jnp.concatenate(taps, axis=1)
    return jnp.dot(
        stacked, conv_weight.reshape(9 * width, width), preferred_element_type=jnp.float32
    )


def normalize(stem):
    mean = jnp.mean(stem, axis=-1, keepdims=True)
    varia = jnp.mean((stem - mean) ** 2, axis=-1, keepdims=True)
    return ((stem - mean) / jnp.sqrt(varia + 1e-05)).astype(jnp.bfloat16)


def attend(normed, qkv_weight):
    length, width = normed.shape
    qkv = jnp.dot(normed, qkv_weight, preferred_element_type=jnp.float32).astype(jnp.bfloat16)
    query = qkv[:, :width].reshape(length, HEADS, HEAD)
    keyed = qkv[:, width : 2 * width].reshape(length, HEADS, HEAD)
    valued = qkv[:, 2 * width :].reshape(length, HEADS, HEAD)
    scores = jnp.einsum("qhd,khd->hqk", query, keyed, preferred_element_type=jnp.float32)
    scores = scores / jnp.sqrt(jnp.float32(HEAD))
    top = jnp.max(scores, axis=-1, keepdims=True)
    expo = jnp.exp(scores - top)
    probs = (expo / jnp.sum(expo, axis=-1, keepdims=True)).astype(jnp.bfloat16)
    mixed = jnp.einsum("hqk,khd->qhd", probs, valued, preferred_element_type=jnp.float32)
    return mixed.astype(jnp.bfloat16).reshape(length, width)


def on_device(field, conv_weight, qkv_weight, out_weight):
    lines = to_lines(field)
    planes, length, _, width = lines.shape
    line = lines.reshape(length, width)
    from_left, from_right = neighbour_lines(line)
    stem = convolve(jnp.stack([from_left, line, from_right]), conv_weight)
    normed = normalize(stem)
    attended = attend(normed, qkv_weight)
    projected = jnp.dot(attended, out_weight, preferred_element_type=jnp.float32)
    result = (stem + projected).astype(jnp.bfloat16)
    return to_blocks(result.reshape(planes, length, 1, width))


def solution(mesh):
    placed = (P(None, "gx", "gy", None), P(), P(), P())
    return jax.shard_map(
        on_device, mesh=mesh, in_specs=placed, out_specs=P(None, "gx", "gy", None), check_vma=False
    )
```

profile of v0, /device:TPU:7, one launch (start us, length us, event | category | flops | bytes accessed | tf_op | source)
XLA Modules:
  0.0 78.3 jit_solution(10470661683168732793)
XLA Ops:
  0.0 1.0 %copy.13 = bf16[1,8,64,128]{3,1,0,2:T(8,128)(2,1)S(1)} copy(bf16[1,8,64,128]{3,2,1,0:T(8,128)(2,1)} %param.4) | data formatting | bytes 262144 | tf_op args[0]
  1.0 29.4 %all_to_all.33 = bf16[1,8,64,128]{3,1,0,2:T(8,128)(2,1)S(1)} all-to-all(bf16[1,8,64,128]{3,1,0,2:T(8,128)(2,1)S(1)} %copy.13), channel_id=1, replica_groups=mesh['gx'=64,'gy'=8] {'gx'}, dimensions={2} | all-to-all | bytes 262144 | tf_op jit(solution)/shard_map/all_to_all | solution.py:11
  30.4 3.2 %collective-permute-start = (bf16[512,128]{1,0:T(8,128)(2,1)S(1)}, bf16[512,128]{1,0:T(8,128)(2,1)S(1)}, u32[]{:S(2)}, u32[]{:S(2)}) collective-permute-start(bf16[512,128]{1,0:T(8,128)(2,1)S(1)} %bitcast.35), channel_id=1, source_target_pairs={{0,8},{8,16},{16,24},{24,32},{32,40},{40,48},{48,56},{56,64},{64,7... | collective-permute-start | bytes 393224 | tf_op jit(solution)/shard_map/ppermute | solution.py:26
  33.7 1.9 %collective-permute-start.1 = (bf16[512,128]{1,0:T(8,128)(2,1)S(1)}, bf16[512,128]{1,0:T(8,128)(2,1)S(1)}, u32[]{:S(2)}, u32[]{:S(2)}) collective-permute-start(bf16[512,128]{1,0:T(8,128)(2,1)S(1)} %bitcast.37), channel_id=1, source_target_pairs={{8,0},{16,8},{24,16},{32,24},{40,32},{48,40},{56,48},{64,56},{72,6... | collective-permute-start | bytes 393224 | tf_op jit(solution)/shard_map/ppermute | solution.py:27
  35.6 0.0 collective-permute-done
  35.7 0.1 maximum_dynamic-update-slice_fusion.4
  35.8 4.4 %collective-permute-done.1 = bf16[512,128]{1,0:T(8,128)(2,1)S(1)} collective-permute-done((bf16[512,128]{1,0:T(8,128)(2,1)S(1)}, bf16[512,128]{1,0:T(8,128)(2,1)S(1)}, u32[]{:S(2)}, u32[]{:S(2)}) %collective-permute-start.1) | collective-permute-done | bytes 131104 | tf_op jit(solution)/shard_map/ppermute | solution.py:27
  40.3 0.1 maximum_dynamic-update-slice_fusion.3
  40.6 0.0 copy-start.2
  40.6 0.5 fusion.21
  41.2 0.1 multiply_reduce_fusion.1
  41.3 0.2 copy-done.2
  41.5 0.3 convolution_convert_fusion
  41.8 3.4 %fusion.22 = (f32[4,512]{1,0:T(4,128)S(1)}, f32[4,512,512]{1,2,0:T(8,128)}) fusion(bf16[512,4,32]{0,2,1:T(8,128)(2,1)S(1)} %bitcast.45, bf16[512,4,32]{0,2,1:T(8,128)(2,1)S(1)} %bitcast.44), kind=kOutput, calls=%fused_computation.38 | convolution fusion | flops 70255104 | bytes 4464640 | tf_op jit(solution)/shard_map/sub | solution.py:60
  45.3 2.7 %fusion.7 = bf16[4,32,512]{2,1,0:T(8,128)(2,1)S(1)} fusion(bf16[512,4,32]{0,2,1:T(8,128)(2,1)S(1)} %bitcast.43, f32[4,512,512]{1,2,0:T(8,128)} %get-tuple-element.23, f32[4,512]{1,0:T(4,128)S(1)} %get-tuple-element.22), kind=kOutput, calls=%fused_computation.10 | convolution fusion | flops 69271552 | bytes 4464640 | tf_op jit(solution)/shard_map/hqk,khd->qhd/dot_general | solution.py:62
  47.9 0.0 copy-done.1
  47.9 0.2 fusion.8
  48.2 0.2 copy.16
  48.3 0.5 broadcast.26
  48.9 1.4 %reduce = bf16[512,128]{1,0:T(8,128)(2,1)S(1)} reduce(bf16[512,1,1,128]{3,2,1,0:T(2,128)(2,1)S(1)} %bitcast.39, bf16[]{:T(256)} %broadcast.26), dimensions={1,2}, to_apply=%bitcast.21.reduce_sub_computation | reduce | bytes 262146
  50.3 0.1 reshape.43
  50.3 27.2 %all_to_all.34 = bf16[64,2,512]{2,1,0:T(2,128)(2,1)S(1)} all-to-all(bf16[64,2,512]{2,1,0:T(2,128)(2,1)S(1)} %reshape.43), channel_id=1, replica_groups=mesh['gx'=64,'gy'=8] {'gx'}, dimensions={0} | all-to-all | bytes 262144 | tf_op jit(solution)/shard_map/all_to_all | solution.py:15
  77.5 0.1 reshape.44
  77.7 0.7 copy.17
  (20 shorter events, 0.5 us)
Async XLA Ops:
  0.0 40.6 %copy-start = (bf16[3,3,128,128]{3,2,1,0:T(8,128)(2,1)S(1)}, bf16[3,3,128,128]{3,2,1,0:T(8,128)(2,1)}, u32[]{:S(2)}) copy-start(bf16[3,3,128,128]{3,2,1,0:T(8,128)(2,1)} %param.5) | copy-start | bytes 884740
  30.4 5.2 %collective-permute-start = (bf16[512,128]{1,0:T(8,128)(2,1)S(1)}, bf16[512,128]{1,0:T(8,128)(2,1)S(1)}, u32[]{:S(2)}, u32[]{:S(2)}) collective-permute-start(bf16[512,128]{1,0:T(8,128)(2,1)S(1)} %bitcast.35), channel_id=1, source_target_pairs={{0,8},{8,16},{16,24},{24,32},{32,40},{40,48},{48,56},{56,64},{64,7... | collective-permute-start | bytes 393224 | tf_op jit(solution)/shard_map/ppermute | solution.py:26
  33.7 6.6 %collective-permute-start.1 = (bf16[512,128]{1,0:T(8,128)(2,1)S(1)}, bf16[512,128]{1,0:T(8,128)(2,1)S(1)}, u32[]{:S(2)}, u32[]{:S(2)}) collective-permute-start(bf16[512,128]{1,0:T(8,128)(2,1)S(1)} %bitcast.37), channel_id=1, source_target_pairs={{8,0},{16,8},{24,16},{32,24},{40,32},{48,40},{56,48},{64,56},{72,6... | collective-permute-start | bytes 393224 | tf_op jit(solution)/shard_map/ppermute | solution.py:27
  40.6 0.9 %copy-start.2 = (bf16[128,384]{1,0:T(8,128)(2,1)S(1)}, bf16[128,384]{1,0:T(8,128)(2,1)}, u32[]{:S(2)}) copy-start(bf16[128,384]{1,0:T(8,128)(2,1)} %param.6) | copy-start | bytes 294916
  45.3 2.7 %copy-start.1 = (bf16[128,128]{1,0:T(8,128)(2,1)S(1)}, bf16[128,128]{1,0:T(8,128)(2,1)}, u32[]{:S(2)}) copy-start(bf16[128,128]{1,0:T(8,128)(2,1)} %param.7) | copy-start | bytes 98308
where the time goes:
time: 78.6 us; the launch traced here: 78.3 us
  blocking collectives  56.6 us (72%)
  matrix products  7.16 us (9%)
  starting transfers between devices  5.12 us (7%)
  waiting for transfers between devices  4.45 us (6%)
  local copies, waits for them, and re-layouts  3.09 us (4%)
  other arithmetic  1.74 us (2%)
    all_to_all x1, blocking collectives, to_lines(): return lax.all_to_all(block, 'gx', split_axis=2, concat_axis=1, tiled=True)  29.4 us
    all_to_all x1, blocking collectives, to_blocks(): return lax.all_to_all(lines, 'gx', split_axis=1, concat_axis=2, tiled=True)  27.2 us
    ppermute x1, waiting for transfers between devices, neighbour_lines(): lax.ppermute(line, ('gx', 'gy'), [(device(c + 1), device(c)) for c in ran...  4.45 us
    sub x1, matrix products, attend(): expo = jnp.exp(scores - top)  3.43 us
    ppermute x1, starting transfers between devices, neighbour_lines(): lax.ppermute(line, ('gx', 'gy'), [(device(c), device(c + 1)) for c in ran...  3.2 us
    dot_general x1, matrix products, attend(): jnp.einsum('hqk,khd->qhd', probs, valued, preferred_element_type=jnp.floa...  2.66 us
    unnamed x14, local copies, waits for them, and re-layouts  2.06 us
    ppermute x1, starting transfers between devices, neighbour_lines(): lax.ppermute(line, ('gx', 'gy'), [(device(c + 1), device(c)) for c in ran...  1.92 us
  transfers between devices with their start and end apart: 2, of which 1 were waited for; matrix products, arithmetic and copies ran while one was open for 0% of the time, Pallas kernels for 0%

commit v1 on v0

--- a/solution.py
+++ b/solution.py
@@ -1,3 +1,4 @@
+import functools
 import jax
 import jax.numpy as jnp
 from jax import lax
@@ -7,12 +8,27 @@
 HEAD = 32
 
 
+def step_on_the_tails(state, on_dim, dim_k):
+    return jnp.concatenate(
+        lax.all_to_all(
+            jnp.stack(jnp.split(state, lax.psum(1, axis_name="gx"), on_dim)),
+            split_axis=0,
+            axis_name="gx",
+            concat_axis=0,
+        ),
+        dim_k,
+    )
+
+
+time_orders = functools.partial(step_on_the_tails, on_dim=1, dim_k=2)
+
+
 def to_lines(block):
     return lax.all_to_all(block, "gx", split_axis=2, concat_axis=1, tiled=True)
 
 
 def to_blocks(lines):
-    return lax.all_to_all(lines, "gx", split_axis=1, concat_axis=2, tiled=True)
+    return time_orders(lines)
 
 
 def neighbour_lines(line):

time: 78.6 us -> 74.5 us (0.948); the launches traced: 78.3 us -> 73.4 us
  waiting for transfers between devices: 4.45 us -> 1.86 us
  blocking collectives: 56.6 us -> 55.2 us
  other arithmetic: 1.74 us -> 0.52 us
    ppermute x1, waiting for transfers between devices: 4.45 us -> 0.01 us  [neighbour_lines(): lax.ppermute(line, ('gx', 'gy'), [(device(c + 1), device(c)) for c in ran...]
    ppermute x1, waiting for transfers between devices: 0.01 us -> 1.86 us  [neighbour_lines(): lax.ppermute(line, ('gx', 'gy'), [(device(c), device(c + 1)) for c in ran...]
    unnamed x6 -> x5, other arithmetic: 1.64 us -> 0.23 us
    all_to_all x1, blocking collectives: 27.2 us -> 25.8 us  [step_on_the_tails(): lax.all_to_all(jnp.stack(jnp.split(state, lax.psum(1, axis_name='gx'), on...]
    unnamed x14 -> x73, local copies, waits for them, and re-layouts: 2.06 us -> 1.72 us
where the time goes in v1:
time: 74.5 us; the launch traced here: 73.4 us
  blocking collectives  55.2 us (74%)
  matrix products  7.34 us (10%)
  starting transfers between devices  5.55 us (7%)
  local copies, waits for them, and re-layouts  2.59 us (3%)
  waiting for transfers between devices  1.86 us (2%)
    all_to_all x1, blocking collectives, to_lines(): return lax.all_to_all(block, 'gx', split_axis=2, concat_axis=1, tiled=True)  29.4 us
    all_to_all x1, blocking collectives, step_on_the_tails(): lax.all_to_all(jnp.stack(jnp.split(state, lax.psum(1, axis_name='gx'), on...  25.8 us
    sub x1, matrix products, attend(): expo = jnp.exp(scores - top)  3.44 us
    ppermute x1, starting transfers between devices, neighbour_lines(): lax.ppermute(line, ('gx', 'gy'), [(device(c), device(c + 1)) for c in ran...  3.26 us
    dot_general x1, matrix products, attend(): jnp.einsum('hqk,khd->qhd', probs, valued, preferred_element_type=jnp.floa...  2.66 us
    ppermute x1, starting transfers between devices, neighbour_lines(): lax.ppermute(line, ('gx', 'gy'), [(device(c + 1), device(c)) for c in ran...  2.29 us
    ppermute x1, waiting for transfers between devices, neighbour_lines(): lax.ppermute(line, ('gx', 'gy'), [(device(c), device(c + 1)) for c in ran...  1.86 us
    unnamed x73, local copies, waits for them, and re-layouts  1.72 us
  transfers between devices with their start and end apart: 2, of which 1 were waited for; matrix products, arithmetic and copies ran while one was open for 0% of the time, Pallas kernels for 0%

profile of v1, /device:TPU:7, one launch (start us, length us, event | category | flops | bytes accessed | tf_op | source)
XLA Modules:
  0.0 73.4 jit_solution(11796493341647624815)
XLA Ops:
  0.0 0.0 copy-start
  0.0 1.0 %copy.10 = bf16[1,8,64,128]{3,1,0,2:T(8,128)(2,1)S(1)} copy(bf16[1,8,64,128]{3,2,1,0:T(8,128)(2,1)} %param.4) | data formatting | bytes 262144 | tf_op args[0]
  1.0 29.4 %all_to_all.20 = bf16[1,8,64,128]{3,1,0,2:T(8,128)(2,1)S(1)} all-to-all(bf16[1,8,64,128]{3,1,0,2:T(8,128)(2,1)S(1)} %copy.10), channel_id=1, replica_groups=mesh['gx'=64,'gy'=8] {'gx'}, dimensions={2} | all-to-all | bytes 262144 | tf_op jit(solution)/shard_map/all_to_all | solution.py:27
  30.4 2.3 %collective-permute-start.1 = (bf16[512,128]{1,0:T(8,128)(2,1)S(1)}, bf16[512,128]{1,0:T(8,128)(2,1)S(1)}, u32[]{:S(2)}, u32[]{:S(2)}) collective-permute-start(bf16[512,128]{1,0:T(8,128)(2,1)S(1)} %bitcast.285), channel_id=1, source_target_pairs={{8,0},{16,8},{24,16},{32,24},{40,32},{48,40},{56,48},{64,56},{72,6... | collective-permute-start | bytes 393224 | tf_op jit(solution)/shard_map/ppermute | solution.py:43
  32.7 3.3 %collective-permute-start = (bf16[512,128]{1,0:T(8,128)(2,1)S(1)}, bf16[512,128]{1,0:T(8,128)(2,1)S(1)}, u32[]{:S(2)}, u32[]{:S(2)}) collective-permute-start(bf16[512,128]{1,0:T(8,128)(2,1)S(1)} %bitcast.286), channel_id=1, source_target_pairs={{0,8},{8,16},{16,24},{24,32},{32,40},{40,48},{48,56},{56,64},{64,7... | collective-permute-start | bytes 393224 | tf_op jit(solution)/shard_map/ppermute | solution.py:42
  36.0 1.9 %collective-permute-done = bf16[512,128]{1,0:T(8,128)(2,1)S(1)} collective-permute-done((bf16[512,128]{1,0:T(8,128)(2,1)S(1)}, bf16[512,128]{1,0:T(8,128)(2,1)S(1)}, u32[]{:S(2)}, u32[]{:S(2)}) %collective-permute-start) | collective-permute-done | bytes 131104 | tf_op jit(solution)/shard_map/ppermute | solution.py:42
  38.0 0.1 constant_dynamic-update-slice_fusion.7
  38.1 0.0 collective-permute-done.1
  38.1 0.1 constant_dynamic-update-slice_fusion.6
  38.4 0.0 copy-start.2
  38.5 0.0 copy-done
  38.5 0.6 fusion.21
  39.1 0.2 multiply_reduce_fusion.1
  39.3 0.0 copy-done.2
  39.3 0.5 convolution_convert_fusion
  39.8 3.4 %fusion.22 = (f32[4,512]{1,0:T(4,128)S(1)}, f32[4,512,512]{1,2,0:T(8,128)}) fusion(bf16[512,4,32]{0,2,1:T(8,128)(2,1)S(1)} %bitcast.293, bf16[512,4,32]{0,2,1:T(8,128)(2,1)S(1)} %bitcast.292), kind=kOutput, calls=%fused_computation.165 | convolution fusion | flops 70255104 | bytes 4464640 | tf_op jit(solution)/shard_map/sub | solution.py:76
  43.3 0.0 copy-start.1
  43.3 2.7 %fusion.7 = bf16[4,32,512]{2,1,0:T(8,128)(2,1)S(1)} fusion(bf16[512,4,32]{0,2,1:T(8,128)(2,1)S(1)} %bitcast.291, f32[4,512,512]{1,2,0:T(8,128)} %get-tuple-element.23, f32[4,512]{1,0:T(4,128)S(1)} %get-tuple-element.22), kind=kOutput, calls=%fused_computation.10 | convolution fusion | flops 69271552 | bytes 4464640 | tf_op jit(solution)/shard_map/hqk,khd->qhd/dot_general | solution.py:78
  45.9 0.0 copy-done.1
  45.9 0.2 fusion.8
  46.9 25.8 %all_to_all.21 = bf16[64,1,8,1,128]{4,2,3,1,0:T(8,128)(2,1)S(1)} all-to-all(bf16[64,1,8,1,128]{4,2,3,1,0:T(8,128)(2,1)S(1)} %constant_dynamic-update-slice_fusion.9), channel_id=1, replica_groups=mesh['gx'=64,'gy'=8] {'gx'}, dimensions={0} | all-to-all | bytes 262144 | tf_op jit(solution)/shard_map/all_to_all | solution.py:13
  72.7 0.7 copy.12
  (80 shorter events, 1.0 us)
Async XLA Ops:
  0.0 38.5 %copy-start = (bf16[3,3,128,128]{3,2,1,0:T(8,128)(2,1)S(1)}, bf16[3,3,128,128]{3,2,1,0:T(8,128)(2,1)}, u32[]{:S(2)}) copy-start(bf16[3,3,128,128]{3,2,1,0:T(8,128)(2,1)} %param.5) | copy-start | bytes 884740
  30.4 7.7 %collective-permute-start.1 = (bf16[512,128]{1,0:T(8,128)(2,1)S(1)}, bf16[512,128]{1,0:T(8,128)(2,1)S(1)}, u32[]{:S(2)}, u32[]{:S(2)}) collective-permute-start(bf16[512,128]{1,0:T(8,128)(2,1)S(1)} %bitcast.285), channel_id=1, source_target_pairs={{8,0},{16,8},{24,16},{32,24},{40,32},{48,40},{56,48},{64,56},{72,6... | collective-permute-start | bytes 393224 | tf_op jit(solution)/shard_map/ppermute | solution.py:43
  32.7 5.2 %collective-permute-start = (bf16[512,128]{1,0:T(8,128)(2,1)S(1)}, bf16[512,128]{1,0:T(8,128)(2,1)S(1)}, u32[]{:S(2)}, u32[]{:S(2)}) collective-permute-start(bf16[512,128]{1,0:T(8,128)(2,1)S(1)} %bitcast.286), channel_id=1, source_target_pairs={{0,8},{8,16},{16,24},{24,32},{32,40},{40,48},{48,56},{56,64},{64,7... | collective-permute-start | bytes 393224 | tf_op jit(solution)/shard_map/ppermute | solution.py:42
  38.4 0.9 %copy-start.2 = (bf16[128,384]{1,0:T(8,128)(2,1)S(1)}, bf16[128,384]{1,0:T(8,128)(2,1)}, u32[]{:S(2)}) copy-start(bf16[128,384]{1,0:T(8,128)(2,1)} %param.6) | copy-start | bytes 294916
  43.3 2.7 %copy-start.1 = (bf16[128,128]{1,0:T(8,128)(2,1)S(1)}, bf16[128,128]{1,0:T(8,128)(2,1)}, u32[]{:S(2)}) copy-start(bf16[128,128]{1,0:T(8,128)(2,1)} %param.7) | copy-start | bytes 98308
